TPU v7x, 32 devices: a whole 2x2x4 slice. The times are simulated.
32 devices in a mesh: dp: 8 (over z, x), tp: 4 (over y, core).
Axes of the slice: x: 2, y: 2, z: 4, core: 2. Of those that a mesh axis runs over, the one named last changes fastest.
Arguments:
- gradients: bfloat16 [8, 4, 5120, 1280], P('dp', None, 'tp'), may hold values from -6 to 6
- right_factor: float32 [4, 1280, 32], replicated, may hold values from -6 to 6
- weights_before: float32 [4, 5120, 1280], P(None, 'tp', 'dp'), may hold values from -0.15625 to 0.15625
- momentum: float32 [4, 5120, 1280], P(None, 'tp', 'dp'), may hold values from -0.3125 to 0.3125
Outputs:
- new_weights: float32 [4, 5120, 1280], P(None, 'tp', 'dp')
- new_basis: float32 [4, 1280, 32], replicated
- new_momentum: float32 [4, 5120, 1280], P(None, 'tp', 'dp')
All inputs are finite; a program needn't handle non-finite values.
Results may differ from a plain program's by a relative error of at most 0.003.
Values sent between devices are 32-bit elements; how exact they have to be, the bound alone decides.
A program may use at most 64 MiB of HBM per device.

v0:
```python
import jax
import jax.numpy as jnp
from jax import lax
from jax.sharding import PartitionSpec as P

RANK = 32


def on_device(gradients, right_factor, weights_before, momentum):
    own_grads = gradients[0]
    part_left = jnp.einsum(
        "liw,lwr->lir",
        own_grads,
        right_factor.astype(jnp.bfloat16),
        preferred_element_type=jnp.float32,
    )
    left = lax.psum(part_left, "dp")
    part_gram = jnp.einsum("lir,lis->lrs", left, left, precision=lax.Precision.HIGHEST)
    small_left = left.astype(jnp.bfloat16)
    gram = lax.psum(part_gram, "tp")
    part_right = jnp.einsum(
        "liw,lir->lwr", own_grads, small_left, preferred_element_type=jnp.float32
    )
    right = lax.psum(part_right, ("dp", "tp"))
    gram = gram + 0.001 * jnp.mean(jnp.diagonal(gram, axis1=1, axis2=2), axis=1)[
        :, None, None
    ] * jnp.eye(RANK, dtype=jnp.float32)
    place = lax.axis_index("dp") * weights_before.shape[2]
    own_right = lax.dynamic_slice_in_dim(right, place, weights_before.shape[2], axis=1)
    root = jnp.linalg.cholesky(gram)
    half = lax.linalg.triangular_solve(
        root, jnp.swapaxes(own_right, 1, 2), left_side=True, lower=True
    )
    mixed = lax.linalg.triangular_solve(root, half, left_side=True, lower=True, transpose_a=True)
    change = jnp.einsum(
        "lir,lrw->liw", left, mixed, precision=lax.Precision.HIGHEST
    ) / lax.axis_size("dp")
    new_momentum = 0.8 * momentum + change
    new_weights = weights_before - 0.05 * new_momentum
    new_basis = right * lax.rsqrt(jnp.mean(right * right, axis=(1, 2), keepdims=True) + 1e-12)
    return (new_weights, new_basis, new_momentum)


def solution(mesh):
    return jax.shard_map(
        on_device,
        mesh=mesh,
        in_specs=(P("dp", None, "tp", None), P(), P(None, "tp", "dp"), P(None, "tp", "dp")),
        out_specs=(P(None, "tp", "dp"), P(), P(None, "tp", "dp")),
        check_vma=False,
    )
```

profile of v0, /device:TPU:0, one launch (start us, length us, event | category | flops | bytes accessed | tf_op | source)
XLA Modules:
  0.0 276.0 jit_solution(18249295536158250338)
XLA Ops:
  7.2 0.0 all-reduce.3.cloned.1.call-start
  7.2 9.6 %fusion.2 = f32[4,1280,32]{1,2,0:T(8,128)} fusion(bf16[1,4,1280,1280]{3,2,1,0:T(8,128)(2,1)} %param.4, f32[4,1280,32]{1,2,0:T(8,128)} %param.5), kind=kOutput, calls=%fused_computation.3 | convolution fusion | flops 419594240 | bytes 14417920 | tf_op jit(solution)/shard_map/liw,lwr->lir/dot_general | solution.py:11
  16.8 0.0 all-reduce.3.cloned.1.call-update
  16.8 0.0 all-reduce.5.cloned.1.call-start
  16.9 0.1 copy.13
  17.0 76.5 %all-reduce.3.cloned.1.call-done = f32[4,1280,32]{1,2,0:T(8,128)} async-done(((f32[4,1280,32]{1,2,0:T(8,128)}), f32[4,1280,32]{1,2,0:T(8,128)}) %all-reduce.3.cloned.1.call-update) | async-done | bytes 655376 | tf_op jit(solution)/shard_map/psum | solution.py:17
  93.4 2.0 fusion.18
  95.5 10.7 %psum.22 = f32[4,32,32]{1,2,0:T(8,128)S(1)} all-reduce(f32[4,32,32]{1,2,0:T(8,128)S(1)} %fusion.18), channel_id=1, replica_groups=mesh['dp'=8,'tp'=4] {'tp'}, use_global_device_ids=true, to_apply=%region_1.0 | all-reduce | flops 4096 | bytes 32768 | tf_op jit(solution)/shard_map/psum | solution.py:20
  106.1 0.5 copy.12
  106.7 0.7 gather_fusion
  107.4 0.1 multiply_add_fusion
  107.5 0.1 copy.14
  107.6 0.1 fusion.15
  107.7 11.7 %custom-call.9 = f32[4,32,32]{2,1,0:T(8,128)S(1)} custom-call(f32[4,32,32]{2,1,0:T(8,128)S(1)} %fusion.15), custom_call_target="Cholesky" | custom-call | tf_op jit(solution)/shard_map/jit(cholesky)/cholesky | solution.py:30
  119.4 8.1 %fusion.5 = f32[4,1280,32]{1,2,0:T(8,128)} fusion(bf16[1,4,1280,1280]{3,2,1,0:T(8,128)(2,1)} %param.4, f32[4,1280,32]{1,2,0:T(8,128)} %all-reduce.3.cloned.1.call-done), kind=kOutput, calls=%fused_computation.8 | convolution fusion | flops 419594240 | bytes 14417920 | tf_op jit(solution)/shard_map/liw,lir->lwr/dot_general | solution.py:21
  127.5 0.0 copy-start
  127.5 0.0 all-reduce.5.cloned.1.call-update
  127.5 0.1 compare_reduce_fusion
  127.7 0.1 select_bitcast_fusion
  127.7 9.8 %custom-call.10 = f32[4,1,32,32]{2,3,1,0:T(8,128)S(1)} custom-call(f32[4,1,32,32]{3,2,1,0:T(8,128)S(1)} %select_bitcast_fusion), custom_call_target="InvertDiagBlocksLowerTriangular" | custom-call | tf_op jit(solution)/shard_map/triangular_solve | solution.py:34
  137.6 119.6 %all-reduce.5.cloned.1.call-done = f32[4,1280,32]{1,2,0:T(8,128)} async-done(((f32[4,1280,32]{1,2,0:T(8,128)}), f32[4,1280,32]{1,2,0:T(8,128)}) %all-reduce.5.cloned.1.call-update) | async-done | bytes 655376 | tf_op jit(solution)/shard_map/psum | solution.py:24
  257.2 1.2 multiply_reduce_fusion
  258.4 1.3 fusion.10
  259.7 0.3 fusion.12
  260.0 2.0 broadcast_multiply_fusion
  262.0 0.0 copy-done
  262.0 7.2 %multiply_subtract_fusion = (f32[4,1280,160]{1,2,0:T(8,128)}, f32[4,1280,160]{1,2,0:T(8,128)}) fusion(f32[4,1280,160]{1,2,0:T(8,128)} %param.6, f32[4,1280,32]{1,2,0:T(8,128)S(1)} %copy-done, f32[4,32,160]{2,1,0:T(8,128)S(1)} %fusion.12, f32[4,1280,160]{1,2,0:T(8,128)} %param.7), kind=kOutput, calls=%fused_computation.7 | convolution fusion | flops 318668800 | bytes 13844480 | tf_op jit(solution)/shard_map/lir,lrw->liw/dot_general | solution.py:35
  (8 shorter events, 0.1 us)
Async XLA Ops:
  7.2 86.3 %all-reduce.3.cloned.1.call-start = ((), (), s32[]{:S(2)}) async-start(), calls=%async_computation | async-start | bytes 1310720 | tf_op jit(solution)/shard_map/psum | solution.py:17
  16.8 240.4 %all-reduce.5.cloned.1.call-start = ((), (), s32[]{:S(2)}) async-start(), calls=%async_computation.1 | async-start | bytes 1310720 | tf_op jit(solution)/shard_map/psum | solution.py:24
  127.5 134.5 %copy-start = (f32[4,1280,32]{1,2,0:T(8,128)S(1)}, f32[4,1280,32]{1,2,0:T(8,128)}, u32[]{:S(2)}) copy-start(f32[4,1280,32]{1,2,0:T(8,128)} %all-reduce.3.cloned.1.call-done) | copy-start | bytes 1966084
Sparse Core Ops, SparseCore 0:
  16.9 76.4 all-reduce.2
  127.6 129.4 all-reduce.4
where the time goes:
time: 276 us
  waiting for transfers between devices  196 us (71%)
  matrix products  28.4 us (10%)
  other arithmetic  25.3 us (9%)
  between operations  14.1 us (5%)
  blocking collectives  10.7 us (4%)
    psum x1, waiting for transfers between devices, on_device(): right = lax.psum(part_right, ('dp', 'tp'))  120 us
    psum x1, waiting for transfers between devices, on_device(): left = lax.psum(part_left, 'dp')  76.5 us
    another operation x4, other arithmetic, on_device(): root = jnp.linalg.cholesky(gram)  11.9 us
    psum x1, blocking collectives, on_device(): gram = lax.psum(part_gram, 'tp')  10.7 us
    another operation x3, other arithmetic, on_device(): lax.linalg.triangular_solve(root, half, left_side=True, lower=True, trans...  9.93 us
    dot_general x1, matrix products, on_device(): jnp.einsum('liw,lwr->lir', own_grads, right_factor.astype(jnp.bfloat16),...  9.56 us
    dot_general x1, matrix products, on_device(): jnp.einsum('liw,lir->lwr', own_grads, small_left, preferred_element_type=...  8.11 us
    dot_general x1, matrix products, on_device(): jnp.einsum('lir,lrw->liw', left, mixed, precision=lax.Precision.HIGHEST)  7.16 us
  transfers between devices with their start and end apart: 2, of which 2 were waited for; matrix products, arithmetic and copies ran while one was open for 4% of the time, Pallas kernels for 0%

commit v1 on v0

--- a/solution.py
+++ b/solution.py
@@ -21,7 +21,8 @@
     part_right = jnp.einsum(
         "liw,lir->lwr", own_grads, small_left, preferred_element_type=jnp.float32
     )
-    right = lax.psum(part_right, ("dp", "tp"))
+    terms = lax.all_gather(part_right, ("dp", "tp"), axis=0, tiled=False)
+    right = terms.sum(axis=0)
     gram = gram + 0.001 * jnp.mean(jnp.diagonal(gram, axis1=1, axis2=2), axis=1)[
         :, None, None
     ] * jnp.eye(RANK, dtype=jnp.float32)

time: 276 us -> 260 us (0.942)
  waiting for transfers between devices: 196 us -> 176 us
  other arithmetic: 25.3 us -> 31.1 us
    psum x1 -> x0, waiting for transfers between devices: 120 us -> none  [on_device(): right = lax.psum(part_right, ('dp', 'tp'))]
    all_gather x0 -> x1, waiting for transfers between devices: none -> 99.2 us  [on_device(): terms = lax.all_gather(part_right, ('dp', 'tp'), axis=0, tiled=False)]
    reduce_sum x0 -> x1, other arithmetic: none -> 8 us  [on_device(): right = terms.sum(axis=0)]
  transfers between devices with their start and end apart: 2 -> 2, of which waited for: 2 -> 2; matrix products, arithmetic and copies ran while one was open for 4% -> 9% of each run, Pallas kernels for 0% -> 0%
where the time goes in v1:
time: 260 us; the launch traced here: 259 us
  waiting for transfers between devices  176 us (68%)
  other arithmetic  31.1 us (12%)
  matrix products  26.2 us (10%)
  between operations  14.1 us (5%)
  blocking collectives  10.7 us (4%)
    all_gather x1, waiting for transfers between devices, on_device(): terms = lax.all_gather(part_right, ('dp', 'tp'), axis=0, tiled=False)  99.2 us
    psum x1, waiting for transfers between devices, on_device(): left = lax.psum(part_left, 'dp')  76.5 us
    another operation x4, other arithmetic, on_device(): root = jnp.linalg.cholesky(gram)  11.9 us
    psum x1, blocking collectives, on_device(): gram = lax.psum(part_gram, 'tp')  10.7 us
    another operation x3, other arithmetic, on_device(): lax.linalg.triangular_solve(root, half, left_side=True, lower=True, trans...  9.94 us
    dot_general x1, matrix products, on_device(): jnp.einsum('liw,lwr->lir', own_grads, right_factor.astype(jnp.bfloat16),...  9.56 us
    dot_general x1, matrix products, on_device(): jnp.einsum('liw,lir->lwr', own_grads, small_left, preferred_element_type=...  8.14 us
    reduce_sum x1, other arithmetic, on_device(): right = terms.sum(axis=0)  8 us
  transfers between devices with their start and end apart: 2, of which 2 were waited for; matrix products, arithmetic and copies ran while one was open for 9% of the time, Pallas kernels for 0%

profile of v1, /device:TPU:0, one launch (start us, length us, event | category | flops | bytes accessed | tf_op | source)
XLA Modules:
  0.0 259.3 jit_solution(10151664990098252630)
XLA Ops:
  7.2 0.0 all-reduce.2.cloned.1.call-start
  7.2 9.6 %fusion.2 = f32[4,1280,32]{1,2,0:T(8,128)} fusion(bf16[1,4,1280,1280]{3,2,1,0:T(8,128)(2,1)} %param.4, f32[4,1280,32]{1,2,0:T(8,128)} %param.5), kind=kOutput, calls=%fused_computation.3 | convolution fusion | flops 419594240 | bytes 14417920 | tf_op jit(solution)/shard_map/liw,lwr->lir/dot_general | solution.py:11
  16.8 0.0 all-reduce.2.cloned.1.call-update
  16.8 0.0 all-gather.3.cloned.1.call-start
  16.8 76.5 %all-reduce.2.cloned.1.call-done = f32[4,1280,32]{1,2,0:T(8,128)} async-done(((f32[4,1280,32]{1,2,0:T(8,128)}), f32[4,1280,32]{1,2,0:T(8,128)}) %all-reduce.2.cloned.1.call-update) | async-done | bytes 655376 | tf_op jit(solution)/shard_map/psum | solution.py:17
  93.3 0.0 copy-start
  93.3 8.1 %fusion.5 = f32[4,1280,32]{1,2,0:T(8,128)} fusion(bf16[1,4,1280,1280]{3,2,1,0:T(8,128)(2,1)} %param.4, f32[4,1280,32]{1,2,0:T(8,128)} %all-reduce.2.cloned.1.call-done), kind=kOutput, calls=%fused_computation.8 | convolution fusion | flops 419594240 | bytes 14417920 | tf_op jit(solution)/shard_map/liw,lir->lwr/dot_general | solution.py:21
  101.5 0.0 all-gather.3.cloned.1.call-update
  101.5 0.1 copy.17
  101.6 0.0 copy-done
  101.6 0.7 fusion.18
  102.3 10.7 %psum.15 = f32[4,32,32]{1,2,0:T(8,128)S(1)} all-reduce(f32[4,32,32]{1,2,0:T(8,128)S(1)} %fusion.18), channel_id=1, replica_groups=mesh['dp'=8,'tp'=4] {'tp'}, use_global_device_ids=true, to_apply=%region_1.0 | all-reduce | flops 4096 | bytes 32768 | tf_op jit(solution)/shard_map/psum | solution.py:20
  113.0 0.5 copy.16
  113.5 0.7 gather_fusion
  114.3 0.1 multiply_add_fusion
  114.4 0.1 copy.18
  114.4 0.1 fusion.15
  114.5 11.7 %custom-call.9 = f32[4,32,32]{2,1,0:T(8,128)S(1)} custom-call(f32[4,32,32]{2,1,0:T(8,128)S(1)} %fusion.15), custom_call_target="Cholesky" | custom-call | tf_op jit(solution)/shard_map/jit(cholesky)/cholesky | solution.py:31
  126.3 0.1 compare_reduce_fusion
  126.4 0.1 select_bitcast_fusion
  126.5 9.8 %custom-call.10 = f32[4,1,32,32]{2,3,1,0:T(8,128)S(1)} custom-call(f32[4,1,32,32]{3,2,1,0:T(8,128)S(1)} %select_bitcast_fusion), custom_call_target="InvertDiagBlocksLowerTriangular" | custom-call | tf_op jit(solution)/shard_map/triangular_solve | solution.py:35
  136.3 99.2 %all-gather.3.cloned.1.call-done = f32[128,1280,32]{1,2,0:T(8,128)} async-done(((f32[4,1280,32]{1,2,0:T(8,128)}), f32[128,1280,32]{1,2,0:T(8,128)}) %all-gather.3.cloned.1.call-update) | async-done | bytes 20971536 | tf_op jit(solution)/shard_map/all_gather | solution.py:24
  235.6 8.0 %reduce_sum.28 = f32[4,1280,32]{1,2,0:T(8,128)S(1)} reduce(f32[32,4,1280,32]{2,3,1,0:T(8,128)} %bitcast.28, f32[]{:T(128)} %constant.68.clone.1), dimensions={0}, to_apply=%region_5.6 | reduce | flops 5079040 | bytes 21626884 | tf_op jit(solution)/shard_map/reduce_sum | solution.py:25
  243.6 0.2 multiply_reduce_fusion
  243.7 0.4 fusion.10
  244.1 0.3 fusion.12
  244.4 1.0 broadcast_multiply_fusion
  245.3 7.2 %multiply_subtract_fusion = (f32[4,1280,160]{1,2,0:T(8,128)}, f32[4,1280,160]{1,2,0:T(8,128)}) fusion(f32[4,1280,160]{1,2,0:T(8,128)} %param.6, f32[4,1280,32]{1,2,0:T(8,128)S(1)} %copy-done, f32[4,32,160]{2,1,0:T(8,128)S(1)} %fusion.12, f32[4,1280,160]{1,2,0:T(8,128)} %param.7), kind=kOutput, calls=%fused_computation.7 | convolution fusion | flops 318668800 | bytes 13844480 | tf_op jit(solution)/shard_map/lir,lrw->liw/dot_general | solution.py:36
  (8 shorter events, 0.1 us)
Async XLA Ops:
  7.2 86.2 %all-reduce.2.cloned.1.call-start = ((), (), s32[]{:S(2)}) async-start(), calls=%async_computation | async-start | bytes 1310720 | tf_op jit(solution)/shard_map/psum | solution.py:17
  16.8 218.8 %all-gather.3.cloned.1.call-start = ((), (), s32[]{:S(2)}) async-start(), calls=%async_computation.1 | async-start | bytes 21626880 | tf_op jit(solution)/shard_map/all_gather | solution.py:24
  93.3 8.3 %copy-start = (f32[4,1280,32]{1,2,0:T(8,128)S(1)}, f32[4,1280,32]{1,2,0:T(8,128)}, u32[]{:S(2)}) copy-start(f32[4,1280,32]{1,2,0:T(8,128)} %all-reduce.2.cloned.1.call-done) | copy-start | bytes 1966084
Sparse Core Ops, SparseCore 0:
  16.9 76.3 all-reduce.1
  101.6 133.9 all-gather.2
